TPU v7x, 32 devices: a whole 2x2x4 slice. The times are simulated.
32 devices in a mesh: dp: 4 (over z), seq: 8 (over y, x, core).
Axes of the slice: x: 2, y: 2, z: 4, core: 2. Of those that a mesh axis runs over, the one named last changes fastest.
Arguments:
- queries: bfloat16 [4, 2048, 512], P('dp', 'seq'), may hold values from -0.890625 to 0.890625
- keys: bfloat16 [4, 2048, 512], P('dp', 'seq'), may hold values from -0.890625 to 0.890625
- values: bfloat16 [4, 2048, 512], P('dp', 'seq'), may hold values from -6 to 6
- level_weights: float32 [4, 6, 4, 2048], P('dp', None, None, 'seq'), may hold values from 0.25 to 4
- proj: bfloat16 [512, 2048], P(None, 'seq'), may hold values from -0.25 to 0.25
- out_grad: bfloat16 [4, 2048, 2048], P('dp', 'seq'), may hold values from -0.59765625 to 0.59765625
Outputs:
- attended_out: bfloat16 [4, 2048, 2048], P('dp', 'seq')
- grad_queries: bfloat16 [4, 2048, 512], P('dp', 'seq')
- grad_keys: bfloat16 [4, 2048, 512], P('dp', 'seq')
- grad_values: bfloat16 [4, 2048, 512], P('dp', 'seq')
- grad_levels: float32 [4, 6, 4, 2048], P('dp', None, None, 'seq')
- grad_proj: float32 [512, 2048], P(None, 'seq')
All inputs are finite; a program needn't handle non-finite values.
Results may differ from a plain program's by a relative error of at most 0.0064.
Values may be sent and summed in bfloat16 or wider, within the bound.
No kernel may reach another device: no remote copies, remote signals or barrier semaphores. Data moves between devices by JAX's collectives and lax.ppermute only.
A program may use at most 64 MiB of HBM per device.

v0:
```python
import jax
import jax.numpy as jnp
from jax import lax
from jax.sharding import PartitionSpec as P


def partner_2(value, axis, stride):
    mask = 2**stride
    pairs = [(source, source ^ mask) for source in range(lax.axis_size(axis))]
    return lax.ppermute(value, axis, pairs)


def level_table(length, stretch, local_bits):
    place = lax.iota(jnp.int32, length)
    blocks = place // stretch
    apart = jnp.bitwise_xor(blocks[:, None], blocks[None, :])
    table = jnp.zeros((length, length), jnp.int32)
    for bit in range(local_bits):
        table = table + (apart >= 1 << bit).astype(jnp.int32)
    causal = place[:, None] >= place[None, :]
    return (table, causal)


def local_weights(lam, table, causal, local_bits):
    weights = jnp.zeros((lam.shape[1], table.shape[0], table.shape[1]), jnp.float32)
    for level in range(local_bits + 1):
        weights = weights + jnp.where(table[None] == level, lam[level][:, :, None], jnp.float32(0))
    return jnp.where(causal[None], weights, jnp.float32(0))


def marked_bit(index, bit):
    return jnp.bitwise_and(jnp.right_shift(index, bit), 1).astype(jnp.float32)


def shards(queries, keys, values, level_weights, proj, out_grad):
    tokens_here = queries.shape[1]
    heads = level_weights.shape[2]
    levels = level_weights.shape[1]
    width = queries.shape[2]
    size = width // heads
    scale = size ** (-0.5)
    span_count = lax.axis_size("seq")
    dev_bits = span_count.bit_length() - 1
    local_bits = levels - 1 - dev_bits
    stretch = tokens_here >> local_bits
    index = lax.axis_index("seq")
    shape = (tokens_here, heads, size)
    query = queries[0].reshape(shape)
    key = keys[0].reshape(shape)
    value = values[0].reshape(shape)
    lam = level_weights[0]
    grad_out = out_grad[0]
    table, causal = level_table(tokens_here, stretch, local_bits)
    scores = jnp.einsum("thd,shd->hts", query, key, preferred_element_type=jnp.float32)
    weights = local_weights(lam, table, causal, local_bits)
    probs = (scale * weights * scores).astype(jnp.bfloat16)
    total = jnp.einsum("hts,shd->thd", probs, value, preferred_element_type=jnp.float32)
    totals = jnp.einsum("shi,shj->hij", key, value, preferred_element_type=jnp.float32)
    running = totals
    states = []
    for bit in range(dev_bits):
        partner = partner_2(running, "seq", bit)
        states.append((marked_bit(index, bit) * partner).astype(jnp.bfloat16))
        running = running + partner
    cross = jnp.zeros_like(total)
    mapped = []
    for bit in range(dev_bits):
        image = jnp.einsum("thi,hij->thj", query, states[bit], preferred_element_type=jnp.float32)
        mapped.append(image)
        cross = cross + lam[local_bits + 1 + bit].T[:, :, None] * image
    attended = (total + scale * cross).astype(jnp.bfloat16).reshape(tokens_here, width)
    full_proj = lax.all_gather(proj, "seq", axis=1, tiled=True)
    out = jnp.dot(attended, full_proj, preferred_element_type=jnp.float32).astype(jnp.bfloat16)
    grad_att = lax.dot_general(
        grad_out, full_proj, (((1,), (1,)), ((), ())), preferred_element_type=jnp.float32
    ).astype(jnp.bfloat16)
    grad_heads = grad_att.reshape(shape)
    dprob = jnp.einsum("thd,shd->hts", grad_heads, value, preferred_element_type=jnp.float32)
    product = jnp.where(causal[None], scale * scores * dprob, jnp.float32(0))
    grads = [
        jnp.sum(jnp.where(table[None] == level, product, jnp.float32(0)), axis=2)
        for level in range(local_bits + 1)
    ]
    dscore = (scale * weights * dprob).astype(jnp.bfloat16)
    grad_q = jnp.einsum("hts,shd->thd", dscore, key, preferred_element_type=jnp.float32)
    grad_k = jnp.einsum("hts,thd->shd", dscore, query, preferred_element_type=jnp.float32)
    grad_v = jnp.einsum("hts,thd->shd", probs, grad_heads, preferred_element_type=jnp.float32)
    updates = []
    for bit in range(dev_bits):
        grads.append(scale * jnp.sum(grad_heads.astype(jnp.float32) * mapped[bit], axis=2).T)
        weighted = (
            scale * lam[local_bits + 1 + bit].T[:, :, None] * grad_heads.astype(jnp.float32)
        ).astype(jnp.bfloat16)
        updates.append(
            jnp.einsum("thi,thj->hij", query, weighted, preferred_element_type=jnp.float32)
        )
        grad_q = grad_q + jnp.einsum(
            "thj,hij->thi", weighted, states[bit], preferred_element_type=jnp.float32
        )
    pending = [marked_bit(index, bit) * updates[bit] for bit in range(dev_bits)]
    carried = jnp.zeros_like(totals)
    for bit in range(dev_bits):
        sending = jnp.stack(pending[bit:])
        arrived = partner_2(sending, "seq", bit)
        carried = carried + (1.0 - marked_bit(index, bit)) * arrived[0]
        for later in range(bit + 1, dev_bits):
            pending[later] = pending[later] + arrived[later - bit]
    returned = carried.astype(jnp.bfloat16)
    grad_k = grad_k + jnp.einsum(
        "shj,hij->shi", value, returned, preferred_element_type=jnp.float32
    )
    grad_v = grad_v + jnp.einsum("shi,hij->shj", key, returned, preferred_element_type=jnp.float32)
    shard = lax.psum_scatter(
        lax.dot_general(
            grad_out, attended, (((0,), (0,)), ((), ())), preferred_element_type=jnp.float32
        ),
        "seq",
        scatter_dimension=0,
        tiled=True,
    )
    shard = lax.psum(shard, "dp")
    grad_levels = jnp.stack(grads)[None]
    return (
        out[None],
        grad_q.astype(jnp.bfloat16).reshape(1, tokens_here, width),
        grad_k.astype(jnp.bfloat16).reshape(1, tokens_here, width),
        grad_v.astype(jnp.bfloat16).reshape(1, tokens_here, width),
        grad_levels,
        shard.T,
    )


def solution(mesh):
    return jax.shard_map(
        shards,
        mesh=mesh,
        in_specs=(
            P("dp", "seq", None),
            P("dp", "seq", None),
            P("dp", "seq", None),
            P("dp", None, None, "seq"),
            P(None, "seq"),
            P("dp", "seq", None),
        ),
        out_specs=(
            P("dp", "seq", None),
            P("dp", "seq", None),
            P("dp", "seq", None),
            P("dp", "seq", None),
            P("dp", None, None, "seq"),
            P(None, "seq"),
        ),
        check_vma=False,
    )
```

profile of v0, /device:TPU:0, one launch (start us, length us, event | category | flops | bytes accessed | tf_op | source)
XLA Modules:
  0.0 157.5 jit_solution(11511535724584984246)
XLA Ops:
  7.2 0.0 copy-start
  7.2 0.0 all-gather.2.cloned.1.call-start
  7.2 0.7 all-gather.2.cloned.1.call-update
  7.9 0.0 reduce-scatter.2.cloned.1.call-start
  8.0 1.0 reshape_squeeze.10
  9.0 0.2 copy.16
  9.2 0.0 copy-start.3
  9.2 1.1 reshape_squeeze.11
  10.3 0.2 fusion.43
  10.5 0.6 collective-permute-start
  11.1 0.1 reshape_squeeze.9
  11.2 0.6 slice_bitcast_fusion.8
  11.8 0.9 fusion.29
  12.7 1.3 fusion.31
  14.0 2.6 %collective-permute-start.1 = (f32[4,128,128]{2,1,0:T(8,128)S(1)}, f32[4,128,128]{2,1,0:T(8,128)S(1)}, u32[]{:S(2)}, u32[]{:S(2)}) collective-permute-start(f32[4,128,128]{2,1,0:T(8,128)S(1)} %add.93), channel_id=1, source_target_pairs={{0,2},{1,3},{2,0},{3,1},{4,6},{5,7},{6,4},{7,5},{8,10},{9,11},{10,... | collective-permute-start | bytes 786440 | tf_op jit(solution)/shard_map/ppermute | solution.py:10
  16.5 0.6 iota_compare_fusion
  17.2 0.3 convolution_bitcast_fusion.10
  17.4 8.0 %collective-permute-done.1 = f32[4,128,128]{2,1,0:T(8,128)S(1)} collective-permute-done((f32[4,128,128]{2,1,0:T(8,128)S(1)}, f32[4,128,128]{2,1,0:T(8,128)S(1)}, u32[]{:S(2)}, u32[]{:S(2)}) %collective-permute-start.1) | collective-permute-done | bytes 262176 | tf_op jit(solution)/shard_map/ppermute | solution.py:10
  25.4 0.7 add.95
  26.1 1.4 collective-permute-start.2
  27.5 1.1 convolution_bitcast_fusion.9
  28.6 14.4 %all-gather.2.cloned.1.call-done = bf16[512,2048]{1,0:T(8,128)(2,1)} async-done(((bf16[512,256]{1,0:T(8,128)(2,1)}), bf16[512,2048]{1,0:T(8,128)(2,1)}) %all-gather.2.cloned.1.call-update) | async-done | bytes 2097168 | tf_op jit(solution)/shard_map/all_gather | solution.py:72
  42.9 3.0 %convolution_convert_fusion.1 = bf16[256,512]{1,0:T(8,128)(2,1)} fusion(bf16[512,2048]{1,0:T(8,128)(2,1)} %all-gather.2.cloned.1.call-done, bf16[1,256,2048]{2,1,0:T(8,128)(2,1)S(1)} %copy-done), kind=kOutput, calls=%fused_computation.21 | convolution fusion | flops 537001984 | bytes 3407872 | tf_op jit(solution)/shard_map/dot_general | solution.py:74
  46.0 1.1 copy.24
  47.2 1.5 fusion.18
  48.7 0.0 copy-done.5
  48.8 0.7 fusion.7
  49.4 2.7 %convolution_bitcast_fusion = f32[2048,512]{0,1:T(8,128)} fusion(bf16[256,512]{0,1:T(8,128)(2,1)S(1)} %bitcast.163, bf16[1,256,2048]{2,1,0:T(8,128)(2,1)S(1)} %copy-done), kind=kOutput, calls=%fused_computation | convolution fusion | flops 536870912 | bytes 5505024 | tf_op jit(solution)/shard_map/dot_general | solution.py:114
  52.1 0.0 reduce-scatter.2.cloned.1.call-update
  52.1 0.0 all-reduce.2.cloned.1.call-start
  52.2 0.6 copy-done.20
  52.8 0.2 fusion.10
  53.1 0.2 convolution_multiply_fusion
  53.3 0.2 convolution_multiply_fusion.1
  53.5 0.1 pad_maximum_fusion
  53.6 0.3 collective-permute-start.3
  53.9 0.1 copy-done.6
  54.1 0.7 select_reduce_fusion
  54.8 0.2 convolution_bitcast_fusion.5
  55.1 0.6 convolution_bitcast_fusion.1
  55.7 0.1 copy-done.15
  55.8 0.0 copy-done.18
  55.9 0.6 convolution_bitcast_fusion.4
  56.5 1.5 fusion.55
  58.0 0.1 fusion.26
  58.1 1.5 collective-permute-start.4
  59.6 0.2 convolution_bitcast_fusion.6
  59.9 0.2 fusion.6
  60.1 12.2 %collective-permute-done.4 = f32[2,4,128,128]{2,3,1,0:T(8,128)S(1)} collective-permute-done((f32[2,4,128,128]{2,3,1,0:T(8,128)S(1)}, f32[2,4,128,128]{2,3,1,0:T(8,128)S(1)}, u32[]{:S(2)}, u32[]{:S(2)}) %collective-permute-start.4) | collective-permute-done | bytes 524320 | tf_op jit(solution)/shard_map/ppermute | solution.py:10
  72.3 0.8 fusion.20
  73.1 0.1 copy-done.10
  73.1 1.1 collective-permute-start.5
  74.3 0.6 copy-done.28
  74.9 0.8 copy.41
  75.7 3.3 %fusion = bf16[1,256,2048]{2,1,0:T(8,128)(2,1)} fusion(bf16[256,512]{0,1:T(8,128)(2,1)S(1)} %bitcast.164, bf16[512,2048]{1,0:T(8,128)(2,1)} %all-gather.2.cloned.1.call-done), kind=kOutput, calls=%fused_computation.2 | convolution fusion | flops 537395200 | bytes 3407872 | tf_op jit(solution)/shard_map/dot_general | solution.py:73
  79.1 29.1 %reduce-scatter.2.cloned.1.call-done = f32[256,512]{0,1:T(8,128)} async-done(((f32[2048,512]{0,1:T(8,128)}), f32[256,512]{0,1:T(8,128)}) %reduce-scatter.2.cloned.1.call-update) | async-done | bytes 524304 | tf_op jit(solution)/shard_map/reduce_scatter | solution.py:113
  108.1 0.0 all-reduce.2.cloned.1.call-update
  108.2 1.1 fusion.45
  109.3 0.3 fusion.9
  109.6 0.8 copy.42
  110.4 0.2 fusion.8
  110.6 0.8 copy.43
  111.5 37.6 %all-reduce.2.cloned.1.call-done = f32[512,256]{1,0:T(8,128)} async-done(((f32[512,256]{1,0:T(8,128)}), f32[512,256]{1,0:T(8,128)}) %all-reduce.2.cloned.1.call-update) | async-done | bytes 524304 | tf_op jit(solution)/shard_map/psum | solution.py:121
  149.1 1.9 %copy.96 = f32[512,256]{1,0:T(8,128)} copy(f32[512,256]{1,0:T(8,128)} %all-reduce.2.cloned.1.call-done) | data formatting | bytes 1048576
  (63 shorter events, 0.2 us)
Async XLA Ops:
  7.2 35.8 %copy-start = (bf16[1,256,2048]{2,1,0:T(8,128)(2,1)S(1)}, bf16[1,256,2048]{2,1,0:T(8,128)(2,1)}, u32[]{:S(2)}) copy-start(bf16[1,256,2048]{2,1,0:T(8,128)(2,1)} %param.11) | copy-start | bytes 3145732
  7.2 3.9 %copy-start.12 = (bf16[1,256,512]{2,1,0:T(8,128)(2,1)S(1)}, bf16[1,256,512]{2,1,0:T(8,128)(2,1)}, u32[]{:S(2)}) copy-start(bf16[1,256,512]{2,1,0:T(8,128)(2,1)} %param.6) | copy-start | bytes 786436
  7.2 4.0 %copy-start.19 = (f32[1,6,4,256]{3,2,1,0:T(4,128)S(1)}, f32[1,6,4,256]{3,2,1,0:T(4,128)}, u32[]{:S(2)}) copy-start(f32[1,6,4,256]{3,2,1,0:T(4,128)} %param.9) | copy-start | bytes 73732
  7.2 35.7 %all-gather.2.cloned.1.call-start = ((), (), s32[]{:S(2)}) async-start(), calls=%async_computation.1 | async-start | bytes 2359296 | tf_op jit(solution)/shard_map/all_gather | solution.py:72
  7.9 100.2 %reduce-scatter.2.cloned.1.call-start = ((), (), s32[]{:S(2)}) async-start(), calls=%async_computation.2 | async-start | bytes 4718592 | tf_op jit(solution)/shard_map/reduce_scatter | solution.py:113
  9.2 1.1 copy-start.3
  10.5 3.4 %collective-permute-start = (f32[4,128,128]{2,1,0:T(8,128)S(1)}, f32[4,128,128]{2,1,0:T(8,128)S(1)}, u32[]{:S(2)}, u32[]{:S(2)}) collective-permute-start(f32[4,128,128]{2,1,0:T(8,128)S(1)} %fusion.43), channel_id=1, source_target_pairs={{0,1},{1,0},{2,3},{3,2},{4,5},{5,4},{6,7},{7,6},{8,9},{9,8},{10,11... | collective-permute-start | bytes 786440 | tf_op jit(solution)/shard_map/ppermute | solution.py:10
  14.0 11.4 %collective-permute-start.1 = (f32[4,128,128]{2,1,0:T(8,128)S(1)}, f32[4,128,128]{2,1,0:T(8,128)S(1)}, u32[]{:S(2)}, u32[]{:S(2)}) collective-permute-start(f32[4,128,128]{2,1,0:T(8,128)S(1)} %add.93), channel_id=1, source_target_pairs={{0,2},{1,3},{2,0},{3,1},{4,6},{5,7},{6,4},{7,5},{8,10},{9,11},{10,... | collective-permute-start | bytes 786440 | tf_op jit(solution)/shard_map/ppermute | solution.py:10
  26.1 21.0 %collective-permute-start.2 = (f32[4,128,128]{2,1,0:T(8,128)}, f32[4,128,128]{2,1,0:T(8,128)S(1)}, u32[]{:S(2)}, u32[]{:S(2)}) collective-permute-start(f32[4,128,128]{2,1,0:T(8,128)} %add.95), channel_id=1, source_target_pairs={{0,4},{1,5},{2,6},{3,7},{4,0},{5,1},{6,2},{7,3},{8,12},{9,13},{10,... | collective-permute-start | bytes 786440 | tf_op jit(solution)/shard_map/ppermute | solution.py:10
  47.1 1.6 %copy-start.1 = (f32[256,4,128]{0,2,1:T(8,128)S(1)}, f32[256,4,128]{0,2,1:T(8,128)}, u32[]{:S(2)}) copy-start(f32[256,4,128]{0,2,1:T(8,128)} %convolution_bitcast_fusion.9) | copy-start | bytes 1572868
  47.1 1.6 %copy-start.5 = (f32[4,256,256]{1,2,0:T(8,128)S(1)}, f32[4,256,256]{1,2,0:T(8,128)}, u32[]{:S(2)}) copy-start(f32[4,256,256]{1,2,0:T(8,128)} %fusion.31) | copy-start | bytes 3145732
  47.1 1.6 %copy-start.13 = (pred[256,256]{0,1:T(8,128)(4,1)S(1)}, pred[256,256]{0,1:T(8,128)(4,1)}, u32[]{:S(2)}) copy-start(pred[256,256]{0,1:T(8,128)(4,1)} %get-tuple-element.31) | copy-start | bytes 196612
  47.1 1.6 %copy-start.16 = (pred[256,256]{0,1:T(8,128)(4,1)S(1)}, pred[256,256]{0,1:T(8,128)(4,1)}, u32[]{:S(2)}) copy-start(pred[256,256]{0,1:T(8,128)(4,1)} %iota_compare_fusion) | copy-start | bytes 196612
  47.1 1.6 %copy-start.21 = (f32[4,256]{1,0:T(4,128)S(1)}, f32[4,256]{1,0:T(4,128)}, u32[]{:S(2)}) copy-start(f32[4,256]{1,0:T(4,128)} %get-tuple-element.25) | copy-start | bytes 12292
  47.1 1.6 %copy-start.23 = (f32[4,256]{1,0:T(4,128)S(1)}, f32[4,256]{1,0:T(4,128)}, u32[]{:S(2)}) copy-start(f32[4,256]{1,0:T(4,128)} %get-tuple-element.26) | copy-start | bytes 12292
  47.1 1.6 %copy-start.25 = (f32[256,4]{0,1:T(4,128)S(1)}, f32[256,4]{0,1:T(4,128)}, u32[]{:S(2)}) copy-start(f32[256,4]{0,1:T(4,128)} %get-tuple-element.24) | copy-start | bytes 12292
  47.1 1.6 %copy-start.26 = (f32[256,4]{0,1:T(4,128)S(1)}, f32[256,4]{0,1:T(4,128)}, u32[]{:S(2)}) copy-start(f32[256,4]{0,1:T(4,128)} %get-tuple-element.27) | copy-start | bytes 12292
  47.1 1.6 %copy-start.27 = (f32[256,4]{0,1:T(4,128)S(1)}, f32[256,4]{0,1:T(4,128)}, u32[]{:S(2)}) copy-start(f32[256,4]{0,1:T(4,128)} %get-tuple-element.28) | copy-start | bytes 12292
  47.2 1.5 copy-start.7
  52.1 0.7 copy-start.20
  52.1 1.8 %copy-start.14 = (pred[256,256]{0,1:T(8,128)(4,1)S(1)}, pred[256,256]{0,1:T(8,128)(4,1)}, u32[]{:S(2)}) copy-start(pred[256,256]{0,1:T(8,128)(4,1)} %get-tuple-element.31) | copy-start | bytes 196612
  52.1 1.8 %copy-start.17 = (pred[256,256]{0,1:T(8,128)(4,1)S(1)}, pred[256,256]{0,1:T(8,128)(4,1)}, u32[]{:S(2)}) copy-start(pred[256,256]{0,1:T(8,128)(4,1)} %iota_compare_fusion) | copy-start | bytes 196612
  52.1 96.9 %all-reduce.2.cloned.1.call-start = ((), (), s32[]{:S(2)}) async-start(), calls=%async_computation.3 | async-start | bytes 1048576 | tf_op jit(solution)/shard_map/psum | solution.py:121
  52.8 1.2 copy-start.6
  53.6 1.2 copy-start.8
  53.6 1.4 copy-start.4
  53.6 1.4 copy-start.22
  53.6 1.4 copy-start.24
  53.6 4.4 %collective-permute-start.3 = (f32[3,4,128,128]{2,3,1,0:T(8,128)S(1)}, f32[3,4,128,128]{2,3,1,0:T(8,128)S(1)}, u32[]{:S(2)}, u32[]{:S(2)}) collective-permute-start(f32[3,4,128,128]{2,3,1,0:T(8,128)S(1)} %pad_maximum_fusion), channel_id=1, source_target_pairs={{0,1},{1,0},{2,3},{3,2},{4,5},{5,4},{6,7},{7,6},{8,9},{9,8},{10,11... | collective-permute-start | bytes 2359304 | tf_op jit(solution)/shard_map/ppermute | solution.py:10
  55.0 0.8 copy-start.15
  55.0 0.9 copy-start.18
  58.0 14.2 %copy-start.2 = (f32[3,4,128,128]{2,3,1,0:T(8,128)}, f32[3,4,128,128]{2,3,1,0:T(8,128)S(1)}, u32[]{:S(2)}) copy-start(f32[3,4,128,128]{2,3,1,0:T(8,128)S(1)} %collective-permute-done.3) | copy-start | bytes 2359300
  58.1 14.1 %collective-permute-start.4 = (f32[2,4,128,128]{2,3,1,0:T(8,128)S(1)}, f32[2,4,128,128]{2,3,1,0:T(8,128)S(1)}, u32[]{:S(2)}, u32[]{:S(2)}) collective-permute-start(f32[2,4,128,128]{2,3,1,0:T(8,128)S(1)} %pad_maximum_fusion.1), channel_id=1, source_target_pairs={{0,2},{1,3},{2,0},{3,1},{4,6},{5,7},{6,4},{7,5},{8,10},{9,11},{10,... | collective-permute-start | bytes 1572872 | tf_op jit(solution)/shard_map/ppermute | solution.py:10
  72.3 0.9 copy-start.10
  73.1 35.0 %collective-permute-start.5 = (f32[1,4,128,128]{2,3,1,0:T(8,128)}, f32[1,4,128,128]{2,3,1,0:T(8,128)}, u32[]{:S(2)}, u32[]{:S(2)}) collective-permute-start(f32[1,4,128,128]{2,3,1,0:T(8,128)} %fusion.20), channel_id=1, source_target_pairs={{0,4},{1,5},{2,6},{3,7},{4,0},{5,1},{6,2},{7,3},{8,12},{9,13},{10,... | collective-permute-start | bytes 786440 | tf_op jit(solution)/shard_map/ppermute | solution.py:10
  74.3 0.6 copy-start.28
  75.7 32.5 %copy-start.11 = (f32[2,4,128,128]{2,3,1,0:T(8,128)S(1)}, f32[2,4,128,128]{2,3,1,0:T(8,128)}, u32[]{:S(2)}) copy-start(f32[2,4,128,128]{2,3,1,0:T(8,128)} %copy-done.10) | copy-start | bytes 1572868
  79.1 31.3 %copy-start.9 = (f32[4,128,256]{2,1,0:T(8,128)S(1)}, f32[4,128,256]{2,1,0:T(8,128)}, u32[]{:S(2)}) copy-start(f32[4,128,256]{2,1,0:T(8,128)} %fusion.55) | copy-start | bytes 1572868
Sparse Core Ops, SparseCore 0:
  9.9 32.9 all-gather.1
  52.2 55.8 reduce-scatter.1
  110.5 38.5 all-reduce.1
where the time goes:
time: 158 us; the launch traced here: 157 us
  waiting for transfers between devices  102 us (65%)
  matrix products  19.2 us (12%)
  between operations  14.2 us (9%)
  local copies, waits for them, and re-layouts  10.2 us (6%)
  starting transfers between devices  7.56 us (5%)
  other arithmetic  4.34 us (3%)
    psum x1, waiting for transfers between devices, shards(): shard = lax.psum(shard, 'dp')  37.6 us
    reduce_scatter x1, waiting for transfers between devices, shards(): lax.psum_scatter(lax.dot_general(grad_out, attended, (((0,), (0,)), ((),...  29.1 us
    ppermute x6, waiting for transfers between devices, partner_2(): return lax.ppermute(value, axis, pairs)  20.1 us
    all_gather x1, waiting for transfers between devices, shards(): full_proj = lax.all_gather(proj, 'seq', axis=1, tiled=True)  14.4 us
    ppermute x6, starting transfers between devices, partner_2(): return lax.ppermute(value, axis, pairs)  7.44 us
    unnamed x65, local copies, waits for them, and re-layouts  6.16 us
    dot_general x1, matrix products, shards(): jnp.dot(attended, full_proj, preferred_element_type=jnp.float32)  3.35 us
  transfers between devices with their start and end apart: 9, of which 5 were waited for; matrix products, arithmetic and copies ran while one was open for 16% of the time, Pallas kernels for 0%

commit v1 on v0

--- a/solution.py
+++ b/solution.py
@@ -2,6 +2,12 @@
 import jax.numpy as jnp
 from jax import lax
 from jax.sharding import PartitionSpec as P
+
+
+def stack_and_merge(array, axis, dim):
+    terms = lax.all_gather(array, axis, axis=0, tiled=False)
+    result = jnp.concatenate(terms, axis=dim)
+    return result
 
 
 def partner_2(value, axis, stride):
@@ -69,7 +75,7 @@
         mapped.append(image)
         cross = cross + lam[local_bits + 1 + bit].T[:, :, None] * image
     attended = (total + scale * cross).astype(jnp.bfloat16).reshape(tokens_here, width)
-    full_proj = lax.all_gather(proj, "seq", axis=1, tiled=True)
+    full_proj = stack_and_merge(proj, "seq", 1)
     out = jnp.dot(attended, full_proj, preferred_element_type=jnp.float32).astype(jnp.bfloat16)
     grad_att = lax.dot_general(
         grad_out, full_proj, (((1,), (1,)), ((), ())), preferred_element_type=jnp.float32

time: 158 us -> 163 us (1.032)
  local copies, waits for them, and re-layouts: 10.2 us -> 15.4 us
  waiting for transfers between devices: 102 us -> 98.4 us
  matrix products: 19.2 us -> 22.5 us
    reshape x0 -> x1, local copies, waits for them, and re-layouts: none -> 2.86 us  [stack_and_merge(): result = jnp.concatenate(terms, axis=dim)]
    unnamed x65 -> x61, local copies, waits for them, and re-layouts: 6.16 us -> 8.37 us
    dot_general x1, matrix products: 3.05 us -> 1.41 us  [shards(): lax.dot_general(grad_out, full_proj, (((1,), (1,)), ((), ())), preferred_...]
  transfers between devices with their start and end apart: 9 -> 9, of which waited for: 5 -> 5; matrix products, arithmetic and copies ran while one was open for 16% -> 19% of each run, Pallas kernels for 0% -> 0%
where the time goes in v1:
time: 163 us; the launch traced here: 162 us
  waiting for transfers between devices  98.4 us (60%)
  matrix products  22.5 us (14%)
  local copies, waits for them, and re-layouts  15.4 us (9%)
  between operations  14.2 us (9%)
  starting transfers between devices  7.94 us (5%)
  other arithmetic  3.56 us (2%)
    psum x1, waiting for transfers between devices, shards(): shard = lax.psum(shard, 'dp')  36.8 us
    reduce_scatter x1, waiting for transfers between devices, shards(): lax.psum_scatter(lax.dot_general(grad_out, attended, (((0,), (0,)), ((),...  28 us
    ppermute x6, waiting for transfers between devices, partner_2(): return lax.ppermute(value, axis, pairs)  19.5 us
    all_gather x1, waiting for transfers between devices, stack_and_merge(): terms = lax.all_gather(array, axis, axis=0, tiled=False)  13.5 us
    unnamed x61, local copies, waits for them, and re-layouts  8.37 us
    ppermute x6, starting transfers between devices, partner_2(): return lax.ppermute(value, axis, pairs)  7.82 us
    dot_general x3, matrix products, shards(): jnp.einsum('thi,hij->thj', query, states[bit], preferred_element_type=jnp...  3.8 us
    dot_general x1, matrix products, shards(): jnp.dot(attended, full_proj, preferred_element_type=jnp.float32)  3.32 us
  transfers between devices with their start and end apart: 9, of which 5 were waited for; matrix products, arithmetic and copies ran while one was open for 19% of the time, Pallas kernels for 0%

profile of v1, /device:TPU:0, one launch (start us, length us, event | category | flops | bytes accessed | tf_op | source)
XLA Modules:
  0.0 162.0 jit_solution(16712970788787160504)
XLA Ops:
  7.2 0.0 copy-start
  7.2 0.0 all-gather.3.cloned.1.call-start
  7.2 0.7 all-gather.3.cloned.1.call-update
  7.9 0.0 reduce-scatter.2.cloned.1.call-start
  8.0 1.0 reshape_squeeze.10
  9.0 0.2 copy.80
  9.2 1.1 reshape_squeeze.11
  10.3 0.0 copy-start.4
  10.3 0.2 fusion.43
  10.6 0.5 copy-done.4
  11.0 0.5 collective-permute-start
  11.5 0.1 reshape_squeeze.9
  11.6 0.6 slice_bitcast_fusion.8
  12.2 0.8 fusion.29
  13.1 1.3 fusion.31
  14.4 2.5 %collective-permute-start.1 = (f32[4,128,128]{2,1,0:T(8,128)S(1)}, f32[4,128,128]{2,1,0:T(8,128)S(1)}, u32[]{:S(2)}, u32[]{:S(2)}) collective-permute-start(f32[4,128,128]{2,1,0:T(8,128)S(1)} %add.93), channel_id=1, source_target_pairs={{0,2},{1,3},{2,0},{3,1},{4,6},{5,7},{6,4},{7,5},{8,10},{9,11},{10,... | collective-permute-start | bytes 786440 | tf_op jit(solution)/shard_map/ppermute | solution.py:16
  16.9 0.7 iota_compare_fusion
  17.6 1.1 convolution_bitcast_fusion.10
  18.7 7.3 %collective-permute-done.1 = f32[4,128,128]{2,1,0:T(8,128)S(1)} collective-permute-done((f32[4,128,128]{2,1,0:T(8,128)S(1)}, f32[4,128,128]{2,1,0:T(8,128)S(1)}, u32[]{:S(2)}, u32[]{:S(2)}) %collective-permute-start.1) | collective-permute-done | bytes 262176 | tf_op jit(solution)/shard_map/ppermute | solution.py:16
  26.0 0.8 add.95
  26.8 1.6 collective-permute-start.2
  28.4 1.1 convolution_bitcast_fusion.9
  29.4 13.5 %all-gather.3.cloned.1.call-done = bf16[4096,256]{1,0:T(8,128)(2,1)} async-done(((bf16[512,256]{1,0:T(8,128)(2,1)}), bf16[4096,256]{1,0:T(8,128)(2,1)}) %all-gather.3.cloned.1.call-update) | async-done | bytes 2097168 | tf_op jit(solution)/shard_map/all_gather | solution.py:8
  42.9 2.9 %copy.88 = bf16[512,8,256]{0,2,1:T(8,128)(2,1)S(1)} copy(bf16[512,8,256]{2,0,1:T(8,128)(2,1)} %bitcast.169) | data formatting | bytes 4194304 | tf_op jit(solution)/shard_map/reshape | solution.py:9
  45.8 1.3 copy-done.1
  47.1 1.4 convolution_convert_fusion.1
  48.6 1.2 copy.89
  49.8 0.0 copy-start.14
  49.8 1.7 %fusion.18 = (f32[256,4]{0,1:T(4,128)S(1)}, f32[256,4]{0,1:T(4,128)S(1)}, f32[256,4]{0,1:T(4,128)S(1)}, f32[256,4,128]{0,2,1:T(8,128)S(1)}) fusion(bf16[256,512]{0,1:T(8,128)(2,1)S(1)} %copy.89, f32[256,4,128]{0,2,1:T(8,128)} %convolution_bitcast_fusion.9, f32[256,4,128]{0,2,1:T(8,128)} %convolution_bitcast_fusion.10, ...), kind=kOutput, calls=%fused_computation.49 | convolution fusion | flops 34599936 | bytes 2371588 | tf_op jit(solution)/shard_map/thi,hij->thj/dot_general | solution.py:74
  51.5 0.7 fusion.7
  52.2 2.7 %convolution_bitcast_fusion = f32[2048,512]{0,1:T(8,128)} fusion(bf16[256,512]{0,1:T(8,128)(2,1)S(1)} %bitcast.170, bf16[1,256,2048]{2,1,0:T(8,128)(2,1)S(1)} %copy-done), kind=kOutput, calls=%fused_computation | convolution fusion | flops 536870912 | bytes 5505024 | tf_op jit(solution)/shard_map/dot_general | solution.py:120
  54.9 0.0 reduce-scatter.2.cloned.1.call-update
  54.9 0.0 all-reduce.2.cloned.1.call-start
  54.9 0.7 copy-done.22
  55.6 0.2 fusion.10
  55.8 0.2 convolution_multiply_fusion
  56.1 0.2 convolution_multiply_fusion.1
  56.3 0.1 pad_maximum_fusion
  56.4 0.3 collective-permute-start.3
  56.7 1.9 %select_reduce_fusion = (f32[4,256]{1,0:T(4,128)S(1)}, f32[4,256]{1,0:T(4,128)S(1)}, f32[4,256]{1,0:T(4,128)S(1)}, f32[4,256,256]{1,2,0:T(8,128)S(1)}) fusion(pred[256,256]{0,1:T(8,128)(4,1)S(1)} %copy-done.19, pred[256,256]{0,1:T(8,128)(4,1)S(1)} %get-tuple-element.42, pred[256,256]{0,1:T(8,128)(4,1)S(1)} %get-tuple-element.41, ...), kind=kOutput, calls=%fused_computation.36 | convolution fusion | flops 69465088 | bytes 2895872 | tf_op jit(solution)/shard_map/thd,shd->hts/dot_general | solution.py:84
  58.6 1.2 convolution_bitcast_fusion.5
  59.8 0.6 convolution_bitcast_fusion.1
  60.5 1.4 convolution_bitcast_fusion.4
  61.9 0.0 copy-done.15
  61.9 1.4 fusion.55
  63.3 0.1 fusion.26
  63.4 1.5 collective-permute-start.4
  65.0 0.2 convolution_bitcast_fusion.6
  65.2 0.2 fusion.6
  65.4 12.2 %collective-permute-done.4 = f32[2,4,128,128]{2,3,1,0:T(8,128)S(1)} collective-permute-done((f32[2,4,128,128]{2,3,1,0:T(8,128)S(1)}, f32[2,4,128,128]{2,3,1,0:T(8,128)S(1)}, u32[]{:S(2)}, u32[]{:S(2)}) %collective-permute-start.4) | collective-permute-done | bytes 524320 | tf_op jit(solution)/shard_map/ppermute | solution.py:16
  77.7 0.7 copy-done.17
  78.4 1.4 collective-permute-start.5
  79.8 0.6 copy-done.26
  80.4 0.8 copy.106
  81.2 3.3 %fusion = bf16[1,256,2048]{2,1,0:T(8,128)(2,1)} fusion(bf16[256,512]{0,1:T(8,128)(2,1)S(1)} %bitcast.171, bf16[512,2048]{0,1:T(8,128)(2,1)} %bitcast.166), kind=kOutput, calls=%fused_computation.2 | convolution fusion | flops 537395200 | bytes 3407872 | tf_op jit(solution)/shard_map/dot_general | solution.py:79
  84.6 28.0 %reduce-scatter.2.cloned.1.call-done = f32[256,512]{0,1:T(8,128)} async-done(((f32[2048,512]{0,1:T(8,128)}), f32[256,512]{0,1:T(8,128)}) %reduce-scatter.2.cloned.1.call-update) | async-done | bytes 524304 | tf_op jit(solution)/shard_map/reduce_scatter | solution.py:119
  112.6 0.0 all-reduce.2.cloned.1.call-update
  112.6 1.0 fusion.45
  113.6 1.3 fusion.9
  114.9 0.8 copy.107
  115.8 0.2 fusion.8
  116.0 0.8 copy.108
  116.9 36.8 %all-reduce.2.cloned.1.call-done = f32[512,256]{1,0:T(8,128)} async-done(((f32[512,256]{1,0:T(8,128)}), f32[512,256]{1,0:T(8,128)}) %all-reduce.2.cloned.1.call-update) | async-done | bytes 524304 | tf_op jit(solution)/shard_map/psum | solution.py:127
  153.6 1.9 %copy.161 = f32[512,256]{1,0:T(8,128)} copy(f32[512,256]{1,0:T(8,128)} %all-reduce.2.cloned.1.call-done) | data formatting | bytes 1048576
  (60 shorter events, 0.3 us)
Async XLA Ops:
  7.2 39.9 %copy-start = (bf16[1,256,2048]{2,1,0:T(8,128)(2,1)S(1)}, bf16[1,256,2048]{2,1,0:T(8,128)(2,1)}, u32[]{:S(2)}) copy-start(bf16[1,256,2048]{2,1,0:T(8,128)(2,1)} %param.11) | copy-start | bytes 3145732
  7.2 4.3 %copy-start.18 = (bf16[1,256,512]{2,1,0:T(8,128)(2,1)S(1)}, bf16[1,256,512]{2,1,0:T(8,128)(2,1)}, u32[]{:S(2)}) copy-start(bf16[1,256,512]{2,1,0:T(8,128)(2,1)} %param.6) | copy-start | bytes 786436
  7.2 4.4 %copy-start.21 = (f32[1,6,4,256]{3,2,1,0:T(4,128)S(1)}, f32[1,6,4,256]{3,2,1,0:T(4,128)}, u32[]{:S(2)}) copy-start(f32[1,6,4,256]{3,2,1,0:T(4,128)} %param.9) | copy-start | bytes 73732
  7.2 35.7 %all-gather.3.cloned.1.call-start = ((), (), s32[]{:S(2)}) async-start(), calls=%async_computation.3 | async-start | bytes 2359296 | tf_op jit(solution)/shard_map/all_gather | solution.py:8
  7.9 104.6 %reduce-scatter.2.cloned.1.call-start = ((), (), s32[]{:S(2)}) async-start(), calls=%async_computation.1 | async-start | bytes 4718592 | tf_op jit(solution)/shard_map/reduce_scatter | solution.py:119
  9.0 5.4 %copy-start.2 = (bf16[256,4,128]{2,1,0:T(4,128)(2,1)}, bf16[256,4,128]{2,1,0:T(4,128)(2,1)S(1)}, u32[]{:S(2)}) copy-start(bf16[256,4,128]{2,1,0:T(4,128)(2,1)S(1)} %reshape_squeeze.10) | copy-start | bytes 786436
  9.2 1.1 copy-start.12
  10.3 0.7 copy-start.4
  11.0 3.3 %collective-permute-start = (f32[4,128,128]{2,1,0:T(8,128)S(1)}, f32[4,128,128]{2,1,0:T(8,128)S(1)}, u32[]{:S(2)}, u32[]{:S(2)}) collective-permute-start(f32[4,128,128]{2,1,0:T(8,128)S(1)} %fusion.43), channel_id=1, source_target_pairs={{0,1},{1,0},{2,3},{3,2},{4,5},{5,4},{6,7},{7,6},{8,9},{9,8},{10,11... | collective-permute-start | bytes 786440 | tf_op jit(solution)/shard_map/ppermute | solution.py:16
  14.3 28.6 %copy-start.8 = (f32[4,128,128]{2,1,0:T(8,128)}, f32[4,128,128]{2,1,0:T(8,128)S(1)}, u32[]{:S(2)}) copy-start(f32[4,128,128]{2,1,0:T(8,128)S(1)} %collective-permute-done) | copy-start | bytes 786436
  14.4 11.6 %collective-permute-start.1 = (f32[4,128,128]{2,1,0:T(8,128)S(1)}, f32[4,128,128]{2,1,0:T(8,128)S(1)}, u32[]{:S(2)}, u32[]{:S(2)}) collective-permute-start(f32[4,128,128]{2,1,0:T(8,128)S(1)} %add.93), channel_id=1, source_target_pairs={{0,2},{1,3},{2,0},{3,1},{4,6},{5,7},{6,4},{7,5},{8,10},{9,11},{10,... | collective-permute-start | bytes 786440 | tf_op jit(solution)/shard_map/ppermute | solution.py:16
  26.0 16.9 %copy-start.6 = (f32[4,128,128]{2,1,0:T(8,128)}, f32[4,128,128]{2,1,0:T(8,128)S(1)}, u32[]{:S(2)}) copy-start(f32[4,128,128]{2,1,0:T(8,128)S(1)} %collective-permute-done.1) | copy-start | bytes 786436
  26.8 23.0 %collective-permute-start.2 = (f32[4,128,128]{2,1,0:T(8,128)}, f32[4,128,128]{2,1,0:T(8,128)}, u32[]{:S(2)}, u32[]{:S(2)}) collective-permute-start(f32[4,128,128]{2,1,0:T(8,128)} %add.95), channel_id=1, source_target_pairs={{0,4},{1,5},{2,6},{3,7},{4,0},{5,1},{6,2},{7,3},{8,12},{9,13},{10,... | collective-permute-start | bytes 786440 | tf_op jit(solution)/shard_map/ppermute | solution.py:16
  45.8 1.3 copy-start.1
  48.5 2.9 %copy-start.5 = (bf16[256,4,128]{2,1,0:T(4,128)(2,1)S(1)}, bf16[256,4,128]{2,1,0:T(4,128)(2,1)}, u32[]{:S(2)}) copy-start(bf16[256,4,128]{2,1,0:T(4,128)(2,1)} %copy-done.4) | copy-start | bytes 786436
  48.5 2.9 %copy-start.10 = (f32[256,4,128]{0,2,1:T(8,128)S(1)}, f32[256,4,128]{0,2,1:T(8,128)}, u32[]{:S(2)}) copy-start(f32[256,4,128]{0,2,1:T(8,128)} %convolution_bitcast_fusion.10) | copy-start | bytes 1572868
  48.5 2.9 %copy-start.11 = (f32[256,4,128]{0,2,1:T(8,128)S(1)}, f32[256,4,128]{0,2,1:T(8,128)}, u32[]{:S(2)}) copy-start(f32[256,4,128]{0,2,1:T(8,128)} %convolution_bitcast_fusion.9) | copy-start | bytes 1572868
  48.5 3.0 %copy-start.19 = (pred[256,256]{0,1:T(8,128)(4,1)S(1)}, pred[256,256]{0,1:T(8,128)(4,1)}, u32[]{:S(2)}) copy-start(pred[256,256]{0,1:T(8,128)(4,1)} %get-tuple-element.43) | copy-start | bytes 196612
  48.5 3.0 %copy-start.20 = (pred[256,256]{0,1:T(8,128)(4,1)S(1)}, pred[256,256]{0,1:T(8,128)(4,1)}, u32[]{:S(2)}) copy-start(pred[256,256]{0,1:T(8,128)(4,1)} %iota_compare_fusion) | copy-start | bytes 196612
  48.5 3.0 %copy-start.23 = (f32[256,4]{0,1:T(4,128)S(1)}, f32[256,4]{0,1:T(4,128)}, u32[]{:S(2)}) copy-start(f32[256,4]{0,1:T(4,128)} %get-tuple-element.36) | copy-start | bytes 12292
  48.6 3.0 %copy-start.24 = (f32[256,4]{0,1:T(4,128)S(1)}, f32[256,4]{0,1:T(4,128)}, u32[]{:S(2)}) copy-start(f32[256,4]{0,1:T(4,128)} %get-tuple-element.39) | copy-start | bytes 12292
  48.6 3.0 %copy-start.25 = (f32[256,4]{0,1:T(4,128)S(1)}, f32[256,4]{0,1:T(4,128)}, u32[]{:S(2)}) copy-start(f32[256,4]{0,1:T(4,128)} %get-tuple-element.40) | copy-start | bytes 12292
  49.8 1.8 %copy-start.14 = (f32[4,256,256]{1,2,0:T(8,128)S(1)}, f32[4,256,256]{1,2,0:T(8,128)}, u32[]{:S(2)}) copy-start(f32[4,256,256]{1,2,0:T(8,128)} %fusion.31) | copy-start | bytes 3145732
  54.9 0.7 copy-start.22
  54.9 98.7 %all-reduce.2.cloned.1.call-start = ((), (), s32[]{:S(2)}) async-start(), calls=%async_computation.2 | async-start | bytes 1048576 | tf_op jit(solution)/shard_map/psum | solution.py:127
  56.3 3.4 %copy-start.13 = (bf16[256,4,128]{0,2,1:T(8,128)(2,1)S(1)}, bf16[256,4,128]{0,2,1:T(8,128)(2,1)}, u32[]{:S(2)}) copy-start(bf16[256,4,128]{0,2,1:T(8,128)(2,1)} %copy-done.12) | copy-start | bytes 786436
  56.4 7.0 %collective-permute-start.3 = (f32[3,4,128,128]{2,3,1,0:T(8,128)S(1)}, f32[3,4,128,128]{2,3,1,0:T(8,128)S(1)}, u32[]{:S(2)}, u32[]{:S(2)}) collective-permute-start(f32[3,4,128,128]{2,3,1,0:T(8,128)S(1)} %pad_maximum_fusion), channel_id=1, source_target_pairs={{0,1},{1,0},{2,3},{3,2},{4,5},{5,4},{6,7},{7,6},{8,9},{9,8},{10,11... | collective-permute-start | bytes 2359304 | tf_op jit(solution)/shard_map/ppermute | solution.py:16
  60.4 1.5 copy-start.15
  63.3 1.6 %copy-start.7 = (f32[4,128,128]{2,1,0:T(8,128)S(1)}, f32[4,128,128]{2,1,0:T(8,128)}, u32[]{:S(2)}) copy-start(f32[4,128,128]{2,1,0:T(8,128)} %copy-done.6) | copy-start | bytes 786436
  63.3 1.8 %copy-start.9 = (f32[4,128,128]{2,1,0:T(8,128)S(1)}, f32[4,128,128]{2,1,0:T(8,128)}, u32[]{:S(2)}) copy-start(f32[4,128,128]{2,1,0:T(8,128)} %copy-done.8) | copy-start | bytes 786436
  63.4 14.2 %collective-permute-start.4 = (f32[2,4,128,128]{2,3,1,0:T(8,128)S(1)}, f32[2,4,128,128]{2,3,1,0:T(8,128)S(1)}, u32[]{:S(2)}, u32[]{:S(2)}) collective-permute-start(f32[2,4,128,128]{2,3,1,0:T(8,128)S(1)} %pad_maximum_fusion.1), channel_id=1, source_target_pairs={{0,2},{1,3},{2,0},{3,1},{4,6},{5,7},{6,4},{7,5},{8,10},{9,11},{10,... | collective-permute-start | bytes 1572872 | tf_op jit(solution)/shard_map/ppermute | solution.py:16
  77.6 0.8 copy-start.17
  78.4 34.2 %collective-permute-start.5 = (f32[1,4,128,128]{2,3,1,0:T(8,128)S(1)}, f32[1,4,128,128]{2,3,1,0:T(8,128)S(1)}, u32[]{:S(2)}, u32[]{:S(2)}) collective-permute-start(f32[1,4,128,128]{2,3,1,0:T(8,128)S(1)} %fusion.20), channel_id=1, source_target_pairs={{0,4},{1,5},{2,6},{3,7},{4,0},{5,1},{6,2},{7,3},{8,12},{9,13},{10,... | collective-permute-start | bytes 786440 | tf_op jit(solution)/shard_map/ppermute | solution.py:16
  79.8 0.6 copy-start.26
  84.6 31.2 %copy-start.3 = (bf16[256,4,128]{2,1,0:T(4,128)(2,1)S(1)}, bf16[256,4,128]{2,1,0:T(4,128)(2,1)}, u32[]{:S(2)}) copy-start(bf16[256,4,128]{2,1,0:T(4,128)(2,1)} %copy-done.2) | copy-start | bytes 786436
  84.6 31.2 %copy-start.16 = (f32[4,128,256]{2,1,0:T(8,128)S(1)}, f32[4,128,256]{2,1,0:T(8,128)}, u32[]{:S(2)}) copy-start(f32[4,128,256]{2,1,0:T(8,128)} %fusion.55) | copy-start | bytes 1572868
Sparse Core Ops, SparseCore 0:
  9.9 32.9 all-gather.2
  55.0 57.5 reduce-scatter.1
  114.9 38.6 all-reduce.1
